TPU v7x, 32 devices: a 4x4x1 block of a 4x4x8 slice. The times are simulated.
32 devices in a mesh: dp: 1 (over z), stage: 32 (over y, x, core).
Axes of the slice: x: 4, y: 4, z: 1, core: 2. Of those that a mesh axis runs over, the one named last changes fastest.
The devices are a block of a 4x4x8 slice.
Arguments:
- x_in: bfloat16 [64, 64, 256], P('dp')
- y_target: bfloat16 [64, 64, 256], P('dp')
- w_up: bfloat16 [32, 256, 1024], P('stage')
- w_down: bfloat16 [32, 1024, 256], P('stage')
- norm_gain: float32 [32, 256], P('stage')
Outputs:
- output 1: float32 [32, 256, 1024], P(('dp', 'stage'))
- output 2: float32 [32, 1024, 256], P(('dp', 'stage'))
- output 3: float32 [32, 256], P(('dp', 'stage'))
- output 4: float32 [1], P('dp')
All inputs are finite; a program needn't handle non-finite values.
Results may differ from a plain program's by a relative error of at most 0.00668016.
Values are sent between devices in bfloat16 or wider.
A program may use at most 768 MiB of HBM per device.

v0:
```python
import functools

import jax
import jax.numpy as jnp
from jax import lax
from jax.experimental import pallas as pl
from jax.experimental.pallas import tpu as pltpu
from jax.sharding import PartitionSpec as P

NORM_EPS = 1e-6
SEG = 8
N_CHUNKS = 4
PIECES = 8
HELP = 2
COLS = 256
BWD_COLS = 128
WEIGHT_COLS = 512
HALF = SEG // 2
GROUP = 4
LATE_ROWS = 2
WRITE_PARTS = 4
GELU_C = 0.7978845608028654
GELU_A = 0.044715
MESH = pl.DeviceIdType.MESH
F32 = jnp.float32
BF16 = jnp.bfloat16


def dot_nn(lhs, rhs):
    return lax.dot_general(lhs, rhs, (((1,), (0,)), ((), ())), preferred_element_type=F32)


def dot_nt(lhs, rhs):
    return lax.dot_general(lhs, rhs, (((1,), (1,)), ((), ())), preferred_element_type=F32)


def dot_tn(lhs, rhs):
    return lax.dot_general(lhs, rhs, (((0,), (0,)), ((), ())), preferred_element_type=F32)


def gelu_gate(hidden):
    sq = hidden * hidden
    gate = 0.5 + 0.5 * jnp.tanh(hidden * (GELU_C + (GELU_C * GELU_A) * sq))
    return gate, sq


def gelu_value(hidden):
    return hidden * gelu_gate(hidden)[0]


def gelu_slope(hidden, gate, sq):
    return gate + ((gate * (1.0 - gate)) * hidden) * (2.0 * GELU_C + (6.0 * GELU_C * GELU_A) * sq)


def inv_rms_of(x_float):
    return lax.rsqrt(jnp.mean(x_float * x_float, axis=-1, keepdims=True) + NORM_EPS)


def fold_rows(block):
    rows, cols = block.shape
    return jnp.sum(block.reshape(rows // 8, 8, cols), axis=0)


def step_kernel(n_stages, loss_scale,
                x_hbm, y_hbm, wu_hbm, wd_hbm, gain_ref,
                dwu_hbm, dwd_hbm, sums_hbm,
                wu, wd, help_u, help_d, gains, acts, grads, hiddens, act_stash, grad_stash, value_stash, slope_stash, targets, dwu, dwd_t, dwd, sums,
                dg_part, dg_stash, loss_part, loss_stash, loss_total,
                load_sem, out_sem, x_sem, y_sem, agu_send, agu_recv, agd_send, agd_recv, hu_send, hu_recv, hd_send, hd_recv, gain_send, gain_recv,
                as_send, as_recv, gs_send, gs_recv, fwd_send, fwd_recv, bwd_send, bwd_recv,
                dg_send, dg_recv, lrow_send, lrow_recv, lcol_send, lcol_recv):
    n_rows = n_stages // SEG
    n_chips = SEG // 2
    chunk = acts.shape[2]
    d_model = acts.shape[3]
    d_ff = wu.shape[2]
    me = lax.axis_index('stage')
    row = lax.div(me, SEG)
    r = lax.rem(me, SEG)
    chip = lax.div(r, 2)
    core = lax.rem(r, 2)
    row_base = row * SEG
    left = lax.rem(chip + n_chips - 1, n_chips) * 2 + core
    right = lax.rem(chip + 1, n_chips) * 2 + core
    across = lax.rem(chip + 2, n_chips) * 2 + core
    flip = 1 - 2 * core
    sib = r + flip

    def rcopy(src, dst, send_sem, recv_sem, dev):
        return pltpu.make_async_remote_copy(src_ref=src, dst_ref=dst, send_sem=send_sem, recv_sem=recv_sem,
                                            device_id={'stage': dev}, device_id_type=MESH)

    load_u = pltpu.make_async_copy(wu_hbm.at[0], wu.at[r], load_sem.at[0])
    load_d = pltpu.make_async_copy(wd_hbm.at[0], wd.at[r], load_sem.at[1])
    load_u.start()
    load_d.start()

    def x_load(k):
        first = pl.multiple_of((r * N_CHUNKS + k) * chunk, chunk)
        return pltpu.make_async_copy(x_hbm.at[pl.ds(first, chunk)], acts.at[0, k], x_sem.at[k])

    def y_load(k):
        first = pl.multiple_of((r * N_CHUNKS + k) * chunk, chunk)
        return pltpu.make_async_copy(y_hbm.at[pl.ds(first, chunk)], targets.at[k], y_sem.at[k])

    @pl.when(row == 0)
    def _():
        for k in range(N_CHUNKS):
            x_load(k).start()

    @pl.when(row == n_rows - 1)
    def _():
        for k in range(N_CHUNKS):
            y_load(k).start()

    gains[r] = jnp.broadcast_to(gain_ref[...], (8, d_model))
    dg_part[...] = jnp.zeros_like(dg_part)
    loss_part[...] = jnp.zeros_like(loss_part)

    with jax.named_scope('barrier'):
        barrier = pltpu.get_barrier_semaphore()
        for step in range(1, SEG):
            pl.semaphore_signal(barrier, inc=1, device_id={'stage': row_base + lax.rem(r + step, SEG)}, device_id_type=MESH)
        for step in range(1, n_rows):
            pl.semaphore_signal(barrier, inc=1, device_id={'stage': lax.rem(row + step, n_rows) * SEG + r}, device_id_type=MESH)
        pl.semaphore_wait(barrier, SEG - 1 + n_rows - 1)

    u_rows = d_model // PIECES
    d_rows = d_ff // PIECES
    helped = row < n_rows // 2
    partner = (n_rows - 1 - row) * SEG + r
    n_help = jnp.where((row == 0) | (row == n_rows - 1), HELP, HELP - 1)
    n_direct = PIECES - n_help
    n_ring = jnp.where(helped, n_direct, PIECES)
    chip_left, chip_right, chip_across = lax.div(left, 2), lax.div(right, 2), lax.div(across, 2)

    def each_piece(first, last, fn):
        def body(piece, carry):
            fn(piece)
            return carry
        lax.fori_loop(first, last, body, 0)

    def u_part(slot, piece):
        return wu.at[slot, pl.ds(pl.multiple_of(piece * u_rows, u_rows), u_rows)]

    def d_part(slot, piece):
        return wd.at[slot, pl.ds(pl.multiple_of(piece * d_rows, d_rows), d_rows)]

    def u_copy(slot, piece, dev):
        part = u_part(slot, piece)
        return rcopy(part, part, agu_send, agu_recv.at[slot, piece], row_base + dev)

    def d_copy(slot, piece, dev):
        part = d_part(slot, piece)
        return rcopy(part, part, agd_send, agd_recv.at[slot, piece], row_base + dev)

    def hu_copy(place, piece, dev):
        part = help_u.at[place, piece]
        return rcopy(part, part, hu_send, hu_recv.at[place, piece], row_base + dev)

    def hd_copy(place, piece, dev):
        part = help_d.at[place, piece]
        return rcopy(part, part, hd_send, hd_recv.at[place, piece], row_base + dev)

    def hu_give(piece):
        rcopy(u_part(r, n_direct + piece), help_u.at[chip, piece], agu_send, hu_recv.at[chip, piece], partner).start()

    def hd_give(piece):
        rcopy(d_part(r, n_direct + piece), help_d.at[chip, piece], agd_send, hd_recv.at[chip, piece], partner).start()

    def hu_return(place, piece):
        slot = place * 2 + core
        rcopy(help_u.at[place, piece], u_part(slot, n_direct + piece), hu_send, agu_recv.at[slot, n_direct + piece], partner).start()

    def hd_return(place, piece):
        slot = place * 2 + core
        rcopy(help_d.at[place, piece], d_part(slot, n_direct + piece), hd_send, agd_recv.at[slot, n_direct + piece], partner).start()

    with jax.named_scope('w_load_u'):
        load_u.wait()
    with jax.named_scope('w_load_d'):
        load_d.wait()
    def ring_first(piece):
        u_copy(r, piece, right).start()
        d_copy(r, piece, left).start()

    def ring_second(piece):
        d_copy(r, piece, right).start()
        u_copy(r, piece, left).start()

    def give(piece):
        hu_give(piece)
        hd_give(piece)

    @pl.when(helped)
    def _():
        each_piece(0, n_help, give)
        each_piece(0, n_direct, ring_first)
        each_piece(0, n_direct, ring_second)

    @pl.when(jnp.logical_not(helped))
    def _():
        each_piece(0, PIECES // 2, ring_first)

    def own_to_sib(piece):
        u_copy(r, piece, sib).start()
        d_copy(r, piece, sib).start()
    each_piece(0, PIECES, own_to_sib)
    for step in range(1, SEG):
        rcopy(gains.at[r], gains.at[r], gain_send, gain_recv, row_base + lax.rem(r + step, SEG)).start()

    @pl.when(jnp.logical_not(helped))
    def _():
        def spread(piece):
            hu_copy(chip, piece, r).wait_recv()
            hu_copy(chip, piece, right).start()
            hu_copy(chip, piece, left).start()
            hd_copy(chip, piece, r).wait_recv()
            hd_copy(chip, piece, left).start()
            hd_copy(chip, piece, right).start()

        def relay(piece):
            hu_copy(chip_left, piece, r).wait_recv()
            hu_copy(chip_left, piece, right).start()
            hu_return(chip_left, piece)
            hd_copy(chip_right, piece, r).wait_recv()
            hd_copy(chip_right, piece, left).start()
            hd_return(chip_right, piece)

        def near(piece):
            hd_copy(chip_left, piece, r).wait_recv()
            hd_return(chip_left, piece)
            hu_copy(chip_right, piece, r).wait_recv()
            hu_return(chip_right, piece)

        def far(piece):
            hu_copy(chip_across, piece, r).wait_recv()
            hu_return(chip_across, piece)
            hd_copy(chip_across, piece, r).wait_recv()
            hd_return(chip_across, piece)

        with jax.named_scope('help'):
            each_piece(0, n_help, spread)
            each_piece(0, n_help, relay)
            each_piece(PIECES // 2, PIECES, ring_first)
            each_piece(0, PIECES, ring_second)
            each_piece(0, n_help, near)
            each_piece(0, n_help, far)

    def relay_near(piece):
        u_copy(left, piece, r).wait_recv()
        u_copy(left, piece, right).start()
        u_copy(left, piece, sib).start()
        d_copy(right, piece, r).wait_recv()
        d_copy(right, piece, left).start()
        d_copy(right, piece, sib).start()

    def take_near(piece):
        d_copy(left, piece, r).wait_recv()
        d_copy(left, piece, sib).start()
        u_copy(right, piece, r).wait_recv()
        u_copy(right, piece, sib).start()

    def take_across(piece):
        u_copy(across, piece, r).wait_recv()
        u_copy(across, piece, sib).start()
        d_copy(across, piece, r).wait_recv()
        d_copy(across, piece, sib).start()

    def take_help(piece):
        for slot in (left, right, across):
            u_copy(slot, piece, r).wait_recv()
            u_copy(slot, piece, sib).start()
            d_copy(slot, piece, r).wait_recv()
            d_copy(slot, piece, sib).start()

    def take_sib(piece):
        for slot in (sib, left + flip, right + flip, across + flip):
            u_copy(slot, piece, r).wait_recv()
            d_copy(slot, piece, r).wait_recv()

    with jax.named_scope('ag_first'):
        each_piece(0, n_ring, relay_near)
    with jax.named_scope('ag_second'):
        each_piece(0, n_ring, take_near)
    with jax.named_scope('ag_across'):
        each_piece(0, n_ring, take_across)
    with jax.named_scope('ag_help'):
        each_piece(n_ring, PIECES, take_help)
    with jax.named_scope('ag_sib'):
        each_piece(0, PIECES, take_sib)
    rcopy(gains.at[pl.ds(0, SEG - 1)], gains.at[pl.ds(0, SEG - 1)], gain_send, gain_recv, me).wait_recv()

    def act_ship(layer, k):
        mine = layer == r
        return rcopy(acts.at[layer, k], act_stash.at[k, jnp.where(mine, SEG, r)], as_send, as_recv.at[k],
                     row_base + jnp.where(mine, sib, layer))

    def grad_ship(layer, k):
        mine = layer == r
        return rcopy(grads.at[layer + 1, k], grad_stash.at[k, jnp.where(mine, SEG, r)], gs_send, gs_recv.at[k],
                     row_base + jnp.where(mine, sib, layer))

    def fwd_layer(layer, k):
        x_float = acts[layer, k].astype(F32)
        normed = (x_float * inv_rms_of(x_float) * gains[layer, 0:1, :]).astype(BF16)
        out = x_float
        for part in range(0, d_ff, COLS):
            cols = slice(part, part + COLS)
            hidden = dot_nn(normed, wu[layer, :, cols])
            hiddens[layer, k, :, cols] = hidden
            out += dot_nn(gelu_value(hidden).astype(BF16), wd[layer, cols, :])
        acts[layer + 1, k] = out.astype(BF16)

    def fwd_input_wait(k):
        @pl.when(row == 0)
        def _():
            x_load(k).wait()

        @pl.when(row > 0)
        def _():
            with jax.named_scope('fwd_wait'):
                rcopy(acts.at[0, k], acts.at[0, k], fwd_send, fwd_recv.at[k], me).wait_recv()

    def top_grad(k):
        y_load(k).wait()
        error_val = acts[SEG, k].astype(F32) - targets[k].astype(F32)
        loss_part[...] += fold_rows(error_val * error_val)
        grads[SEG, k] = ((2.0 * loss_scale) * error_val).astype(BF16)

    def fwd_group(group, k):
        for step in range(GROUP):
            fwd_layer(group * GROUP + step, k)
        return k

    def fwd_chunk(k, carry):
        fwd_input_wait(k)
        with jax.named_scope('fwd_layers'):
            lax.fori_loop(0, SEG // GROUP, fwd_group, k)

        @pl.when(row < n_rows - 1)
        def _():
            rcopy(acts.at[SEG, k], acts.at[0, k], fwd_send, fwd_recv.at[k], me + SEG).start()
        for layer in range(SEG):
            act_ship(layer, k).start()

        @pl.when(row == n_rows - 1)
        def _():
            top_grad(k)
        return carry

    lax.fori_loop(0, jnp.where(row == n_rows - 1, 1, N_CHUNKS), fwd_chunk, 0)

    def bwd_layer(step, k, joined):
        layer = SEG - 1 - step
        grad_out = grads[layer + 1, k]
        x_float = acts[layer, k].astype(F32)
        inv_rms = inv_rms_of(x_float)
        x_hat = x_float * inv_rms
        gain = gains[layer, 0:1, :]
        grad_normed = 0.0
        pieces = []
        for part in range(0, d_ff, BWD_COLS):
            cols = slice(part, part + BWD_COLS)
            hidden = hiddens[layer, k, :, cols]
            slope = gelu_slope(hidden, *gelu_gate(hidden))
            grad_gelu = dot_nt(grad_out, wd[layer, cols, :]).astype(BF16).astype(F32)
            pieces.append((grad_gelu * slope).astype(BF16))
            if not joined:
                grad_normed += dot_nt(pieces[-1], wu[layer, :, cols])
        if joined:
            grad_normed = dot_nt(jnp.concatenate(pieces, axis=1), wu[layer])
        grad_normed = grad_normed.astype(BF16).astype(F32)
        dg_part[layer] += fold_rows(grad_normed * x_hat)
        grad_hat = grad_normed * gain
        mean_dot = jnp.mean(grad_hat * x_hat, axis=-1, keepdims=True)
        grad_x = inv_rms * (grad_hat - x_hat * mean_dot)
        grads[layer, k] = (grad_out.astype(F32) + grad_x).astype(BF16)

    def bwd_group(group, k):
        for step in range(GROUP):
            bwd_layer(group * GROUP + step, k, joined=True)

        @pl.when((row > 0) & (group == SEG // GROUP - 1))
        def _():
            rcopy(grads.at[0, k], grads.at[SEG, k], bwd_send, bwd_recv.at[k], me - SEG).start()
        for step in range(GROUP):
            grad_ship(SEG - 1 - group * GROUP - step, k).start()
        return k

    def both_group(group, k):
        for step in range(GROUP):
            bwd_layer(group * GROUP + step, k - 1, joined=False)
            fwd_layer(group * GROUP + step, k)

        @pl.when((row > 0) & (group == SEG // GROUP - 1))
        def _():
            rcopy(grads.at[0, k - 1], grads.at[SEG, k - 1], bwd_send, bwd_recv.at[k - 1], me - SEG).start()
        for step in range(GROUP):
            grad_ship(SEG - 1 - group * GROUP - step, k - 1).start()
        return k

    def both_chunks(k, carry):
        fwd_input_wait(k)
        with jax.named_scope('both_layers'):
            lax.fori_loop(0, SEG // GROUP, both_group, k)
        top_grad(k)
        for layer in range(SEG):
            act_ship(layer, k).start()
        return carry

    @pl.when(row == n_rows - 1)
    def _():
        lax.fori_loop(1, N_CHUNKS, both_chunks, 0)
        loss_stash[r] = loss_part[...]
        for step in range(1, SEG):
            rcopy(loss_stash.at[r], loss_stash.at[r], lrow_send, lrow_recv, row_base + lax.rem(r + step, SEG)).start()

    rest = act_stash.at[0, pl.ds(0, SEG)]
    all_rest = acts.at[pl.ds(0, SEG)]

    def owner_block(index):
        return lax.div(index, 2), pl.ds(lax.rem(index, 2) * HALF, HALF)

    def value_block(index, carry):
        k, srcs = owner_block(index)

        @pl.when(lax.rem(index, 2) == 0)
        def _():
            with jax.named_scope('as_wait'):
                rcopy(rest, rest, as_send, as_recv.at[k], me).wait_recv()
            act_stash[k, r] = acts[r, k]
        x_float = act_stash[k, srcs].reshape(HALF * chunk, d_model).astype(F32)
        normed = (x_float * inv_rms_of(x_float) * gains[r, 0:1, :]).astype(BF16)
        act_stash[k, srcs] = normed.reshape(HALF, chunk, d_model)
        for part in range(0, d_ff, COLS):
            cols = slice(part, part + COLS)
            hidden = dot_nn(normed, wu[r, :, cols])
            gate, sq = gelu_gate(hidden)
            value_stash[k, srcs, :, cols] = (hidden * gate).astype(BF16).reshape(HALF, chunk, COLS)
            slope_stash[k, srcs, :, cols] = gelu_slope(hidden, gate, sq).reshape(HALF, chunk, COLS)
        return carry

    def sent_own(piece):
        rcopy(u_part(r, 0), u_part(r, 0), agu_send, gain_recv, me).wait_send()
        rcopy(d_part(r, 0), d_part(r, 0), agd_send, gain_recv, me).wait_send()

    def sent_help(piece):
        rcopy(help_u.at[0, 0], help_u.at[0, 0], hu_send, gain_recv, me).wait_send()
        rcopy(help_d.at[0, 0], help_d.at[0, 0], hd_send, gain_recv, me).wait_send()

    def value_phase():
        dwu[...] = jnp.zeros_like(dwu)
        dwd_t[...] = jnp.zeros_like(dwd_t)
        with jax.named_scope('value_blocks'):
            lax.fori_loop(0, 2 * N_CHUNKS, value_block, 0)
        each_piece(0, jnp.where(helped, 3 * n_direct + n_help + 4 * PIECES, 7 * PIECES), sent_own)
        each_piece(0, jnp.where(helped, 0, 6 * n_help), sent_help)
        rest_gain = gains.at[pl.ds(0, SEG - 1)]
        rcopy(rest_gain, rest_gain, gain_send, gain_recv, me).wait_send()
        rcopy(all_rest, all_rest, as_send, dg_recv, me).wait_send()

        @pl.when(row < n_rows - 1)
        def _():
            rcopy(acts.at[0], acts.at[0], fwd_send, dg_recv, me).wait_send()

    @pl.when(row < n_rows - LATE_ROWS)
    def _():
        value_phase()

    def weight_block(k, carry):
        rows = SEG * chunk
        with jax.named_scope('gs_wait'):
            rcopy(rest, rest, gs_send, gs_recv.at[k], me).wait_recv()
        grad_stash[k, r] = grads[r + 1, k]
        normed = act_stash[k, pl.ds(0, SEG)].reshape(rows, d_model)
        grad_out = grad_stash[k, pl.ds(0, SEG)].reshape(rows, d_model)
        for part in range(0, d_ff, WEIGHT_COLS):
            cols = slice(part, part + WEIGHT_COLS)
            dwd_t[:, cols] += dot_tn(grad_out, value_stash[k, :, :, cols].reshape(rows, WEIGHT_COLS))
            grad_gelu = dot_nt(grad_out, wd[r, cols, :]).astype(BF16).astype(F32)
            grad_hidden = (grad_gelu * slope_stash[k, :, :, cols].reshape(rows, WEIGHT_COLS)).astype(BF16)
            dwu[:, cols] += dot_tn(normed, grad_hidden)
        return carry

    def bwd_chunk(k, carry):
        @pl.when(row < n_rows - 1)
        def _():
            with jax.named_scope('bwd_wait'):
                rcopy(grads.at[SEG, k], grads.at[SEG, k], bwd_send, bwd_recv.at[k], me).wait_recv()

        with jax.named_scope('bwd_layers'):
            lax.fori_loop(0, SEG // GROUP, bwd_group, k)
        return carry

    lax.fori_loop(jnp.where(row == n_rows - 1, N_CHUNKS - 1, 0), N_CHUNKS, bwd_chunk, 0)

    def dg_ship(layer):
        return rcopy(dg_part.at[layer], dg_stash.at[r], dg_send, dg_recv, row_base + layer)

    for step in range(1, SEG):
        dg_ship(lax.rem(r + step, SEG)).start()
    dg_stash[r] = dg_part[r]

    @pl.when(row >= n_rows - LATE_ROWS)
    def _():
        value_phase()

    with jax.named_scope('weight_blocks'):
        lax.fori_loop(0, N_CHUNKS, weight_block, 0)
    @pl.when(row == n_rows - 1)
    def _():
        rest_row = loss_stash.at[pl.ds(0, SEG - 1)]
        rcopy(rest_row, rest_row, lrow_send, lrow_recv, me).wait_recv()
        loss_total[...] = jnp.sum(loss_stash[...], axis=0)
        for step in range(1, n_rows):
            rcopy(loss_total, loss_total, lcol_send, lcol_recv, me - step * SEG).start()

    with jax.named_scope('turn'):
        up_out = pltpu.make_async_copy(dwu, dwu_hbm.at[0], out_sem.at[0])
        up_out.start()
        dwd[...] = dwd_t[...].T
        down_out = pltpu.make_async_copy(dwd, dwd_hbm.at[0], out_sem.at[1])
        down_out.start()

    rest_dg = dg_stash.at[pl.ds(0, SEG - 1)]
    with jax.named_scope('dg_wait'):
        rcopy(rest_dg, rest_dg, dg_send, dg_recv, me).wait_recv()
    sums[0:8] = jnp.sum(dg_stash[...], axis=0)

    @pl.when(row < n_rows - 1)
    def _():
        rcopy(loss_total, loss_total, lcol_send, lcol_recv, me).wait_recv()
    sums[8:16] = loss_total[...]
    sums_out = pltpu.make_async_copy(sums, sums_hbm, out_sem.at[2])
    sums_out.start()

    rcopy(all_rest, all_rest, gs_send, dg_recv, me).wait_send()
    rcopy(rest_dg, rest_dg, dg_send, dg_recv, me).wait_send()

    @pl.when(row > 0)
    def _():
        rcopy(grads.at[0], grads.at[0], bwd_send, dg_recv, me).wait_send()

    @pl.when(row == n_rows - 1)
    def _():
        rest_row = loss_stash.at[pl.ds(0, SEG - 1)]
        rcopy(rest_row, rest_row, lrow_send, lrow_recv, me).wait_send()
        for step in range(1, n_rows):
            rcopy(loss_total, loss_total, lcol_send, lcol_recv, me).wait_send()
    up_out.wait()
    down_out.wait()
    sums_out.wait()


def write_kernel(n_parts, loss_scale, up_hbm, down_hbm, sums_hbm, up_out, down_out, gain_out, loss_out,
                 up_buf, down_buf, sums_buf, gain_buf, loss_buf, in_sem, out_sem, small_sem):
    pairs = ((up_hbm, up_buf, up_out), (down_hbm, down_buf, down_out))

    def part(ref, index):
        rows = ref.shape[0] // n_parts
        return ref.at[pl.ds(index * rows, rows)]

    sums_read = pltpu.make_async_copy(sums_hbm, sums_buf, small_sem.at[0])
    gain_write = pltpu.make_async_copy(gain_buf, gain_out, small_sem.at[1])
    loss_write = pltpu.make_async_copy(loss_buf, loss_out, small_sem.at[2])
    sums_read.start()
    reads, writes = [], []
    for side, (src, buf, dst) in enumerate(pairs):
        for index in range(n_parts):
            reads.append(pltpu.make_async_copy(part(src.at[0], index), part(buf, index), in_sem.at[side, index]))
            writes.append(pltpu.make_async_copy(part(buf, index), part(dst.at[0], index), out_sem.at[side, index]))
    for read in reads:
        read.start()
    sums_read.wait()
    gain_buf[...] = jnp.sum(sums_buf[0:8], axis=0, keepdims=True)
    loss_buf[0] = jnp.sum(sums_buf[8:16]) * loss_scale
    for read, write in zip(reads, writes):
        read.wait()
        write.start()
    gain_write.start()
    loss_write.start()
    for write in writes:
        write.wait()
    gain_write.wait()
    loss_write.wait()


def solution(mesh):
    n_stages = mesh.shape['stage']

    def stage_body(x_in, y_target, w_up, w_down, norm_gain):
        n_micro, n_tok, d_model = x_in.shape
        d_ff = w_up.shape[2]
        n_rows = n_micro * n_tok
        chunk = n_rows // SEG // N_CHUNKS
        loss_scale = 1.0 / (n_rows * d_model)
        sem = pltpu.SemaphoreType.DMA
        act_shape = (N_CHUNKS, chunk, d_model)
        scratch = [
            pltpu.VMEM((SEG, d_model, d_ff), BF16),
            pltpu.VMEM((SEG, d_ff, d_model), BF16),
            pltpu.VMEM((SEG // 2, HELP, d_model // PIECES, d_ff), BF16),
            pltpu.VMEM((SEG // 2, HELP, d_ff // PIECES, d_model), BF16),
            pltpu.VMEM((SEG, 8, d_model), F32),
            pltpu.VMEM((SEG + 1,) + act_shape, BF16),
            pltpu.VMEM((SEG + 1,) + act_shape, BF16),
            pltpu.VMEM((SEG, N_CHUNKS, chunk, d_ff), F32),
            pltpu.VMEM((N_CHUNKS, SEG + 1, chunk, d_model), BF16),
            pltpu.VMEM((N_CHUNKS, SEG + 1, chunk, d_model), BF16),
            pltpu.VMEM((N_CHUNKS, SEG, chunk, d_ff), BF16),
            pltpu.VMEM((N_CHUNKS, SEG, chunk, d_ff), F32),
            pltpu.VMEM(act_shape, BF16),
            pltpu.VMEM((d_model, d_ff), F32),
            pltpu.VMEM((d_model, d_ff), F32),
            pltpu.VMEM((d_ff, d_model), F32),
            pltpu.VMEM((16, d_model), F32),
            pltpu.VMEM((SEG, 8, d_model), F32),
            pltpu.VMEM((SEG, 8, d_model), F32),
            pltpu.VMEM((8, d_model), F32),
            pltpu.VMEM((SEG, 8, d_model), F32),
            pltpu.VMEM((8, d_model), F32),
            sem((2,)), sem((3,)), sem((N_CHUNKS,)), sem((N_CHUNKS,)),
            sem, sem((SEG, PIECES)), sem, sem((SEG, PIECES)), sem, sem((SEG // 2, HELP)), sem, sem((SEG // 2, HELP)), sem, sem,
            sem, sem((N_CHUNKS,)), sem, sem((N_CHUNKS,)), sem, sem((N_CHUNKS,)), sem, sem((N_CHUNKS,)),
            sem, sem, sem, sem, sem, sem,
        ]
        any_spec = pl.BlockSpec(memory_space=pl.ANY)
        vmem_spec = pl.BlockSpec(memory_space=pltpu.VMEM)
        dw_up, dw_down, sums = pl.pallas_call(
            functools.partial(step_kernel, n_stages, loss_scale),
            out_shape=(jax.ShapeDtypeStruct(w_up.shape, F32), jax.ShapeDtypeStruct(w_down.shape, F32),
                       jax.ShapeDtypeStruct((16, d_model), F32)),
            in_specs=[any_spec, any_spec, any_spec, any_spec, vmem_spec],
            out_specs=(any_spec, any_spec, any_spec),
            scratch_shapes=scratch,
            compiler_params=pltpu.CompilerParams(collective_id=0, has_side_effects=True,
                                                 vmem_limit_bytes=67043328),
        )(x_in.reshape(n_rows, d_model), y_target.reshape(n_rows, d_model), w_up, w_down, norm_gain)
        return pl.pallas_call(
            functools.partial(write_kernel, WRITE_PARTS, loss_scale),
            out_shape=(jax.ShapeDtypeStruct(w_up.shape, F32), jax.ShapeDtypeStruct(w_down.shape, F32),
                       jax.ShapeDtypeStruct(norm_gain.shape, F32), jax.ShapeDtypeStruct((1,), F32)),
            in_specs=[any_spec, any_spec, any_spec],
            out_specs=(any_spec, any_spec, any_spec, any_spec),
            scratch_shapes=[pltpu.VMEM(w_up.shape[1:], F32), pltpu.VMEM(w_down.shape[1:], F32),
                            pltpu.VMEM((16, d_model), F32), pltpu.VMEM((1, d_model), F32), pltpu.SMEM((1,), F32),
                            sem((2, WRITE_PARTS)), sem((2, WRITE_PARTS)), sem((3,))],
        )(dw_up, dw_down, sums)

    return jax.shard_map(stage_body, mesh=mesh,
                         in_specs=(P('dp'), P('dp'), P('stage'), P('stage'), P('stage')),
                         out_specs=(P(('dp', 'stage')), P(('dp', 'stage')), P(('dp', 'stage')), P('dp')),
                         check_vma=False)
```

profile of v0, /device:TPU:97, one launch (start us, length us, event | category | flops | bytes accessed | tf_op | source)
XLA Modules:
  0.0 125.7 jit_solution(15606551089933913765)
XLA Ops:
  0.6 122.2 %shard_map.84 = (f32[1,256,1024]{2,1,0:T(8,128)}, f32[1,1024,256]{2,1,0:T(8,128)}, f32[16,256]{1,0:T(8,128)}) custom-call(bf16[4096,256]{1,0:T(8,128)(2,1)} %bitcast.2, bf16[4096,256]{1,0:T(8,128)(2,1)} %bitcast.3, bf16[1,256,1024]{2,1,0:T(8,128)(2,1)} %wu_hbm.1, bf16[1,1024,256]{2,1,0:T(8,128)(2,1)} %wd_hbm.1, f32[1,256]{1,0:T(1,128)} %gain_ref.1), custom_call_target="tpu_custom_call" | custom-call | tf_op jit(solution)/shard_map/pallas_call | solution.py:630
  122.8 2.9 %shard_map.85 = (f32[1,256,1024]{2,1,0:T(8,128)}, f32[1,1024,256]{2,1,0:T(8,128)}, f32[1,256]{1,0:T(1,128)}, f32[1]{0:T(128)}) custom-call(f32[1,256,1024]{2,1,0:T(8,128)} %get-tuple-element.7.up_hbm, f32[1,1024,256]{2,1,0:T(8,128)} %get-tuple-element.8.down_hbm, f32[16,256]{1,0:T(8,128)} %get-tuple-element.9.sums_hbm), custom_call_target="tpu_custom_call" | custom-call | tf_op jit(solution)/shard_map/pallas_call | solution.py:640
where the time goes:
time: 126 us
  Pallas kernels  125 us (99%)
    pallas_call x1, Pallas kernels, stage_body(): pl.pallas_call(functools.partial(step_kernel, n_stages, loss_scale), out_...  122 us
    pallas_call x1, Pallas kernels, stage_body(): pl.pallas_call(functools.partial(write_kernel, WRITE_PARTS, loss_scale),...  2.87 us

commit v1 on v0

--- a/solution.py
+++ b/solution.py
@@ -13,6 +13,7 @@
 PIECES = 8
 HELP = 2
 COLS = 256
+FWD_COLS = 256
 BWD_COLS = 128
 WEIGHT_COLS = 512
 HALF = SEG // 2
@@ -301,16 +302,21 @@
         return rcopy(grads.at[layer + 1, k], grad_stash.at[k, jnp.where(mine, SEG, r)], gs_send, gs_recv.at[k],
                      row_base + jnp.where(mine, sib, layer))
 
-    def fwd_layer(layer, k):
+    def fwd_layer(layer, k, joined):
         x_float = acts[layer, k].astype(F32)
         normed = (x_float * inv_rms_of(x_float) * gains[layer, 0:1, :]).astype(BF16)
-        out = x_float
-        for part in range(0, d_ff, COLS):
-            cols = slice(part, part + COLS)
+        values = []
+        update = 0.0
+        for part in range(0, d_ff, FWD_COLS):
+            cols = slice(part, part + FWD_COLS)
             hidden = dot_nn(normed, wu[layer, :, cols])
             hiddens[layer, k, :, cols] = hidden
-            out += dot_nn(gelu_value(hidden).astype(BF16), wd[layer, cols, :])
-        acts[layer + 1, k] = out.astype(BF16)
+            values.append(gelu_value(hidden).astype(BF16))
+            if not joined:
+                update += dot_nn(values[-1], wd[layer, cols, :])
+        if joined:
+            update = dot_nn(jnp.concatenate(values, axis=1), wd[layer])
+        acts[layer + 1, k] = (x_float + update).astype(BF16)
 
     def fwd_input_wait(k):
         @pl.when(row == 0)
@@ -330,7 +336,7 @@
 
     def fwd_group(group, k):
         for step in range(GROUP):
-            fwd_layer(group * GROUP + step, k)
+            fwd_layer(group * GROUP + step, k, joined=True)
         return k
 
     def fwd_chunk(k, carry):
@@ -391,7 +397,7 @@
     def both_group(group, k):
         for step in range(GROUP):
             bwd_layer(group * GROUP + step, k - 1, joined=False)
-            fwd_layer(group * GROUP + step, k)
+            fwd_layer(group * GROUP + step, k, joined=False)
 
         @pl.when((row > 0) & (group == SEG // GROUP - 1))
         def _():

time: 126 us -> 125 us (level)
  no operation moved by 1% of the time
where the time goes in v1:
time: 125 us
  Pallas kernels  124 us (99%)
    pallas_call x1, Pallas kernels, stage_body(): pl.pallas_call(functools.partial(step_kernel, n_stages, loss_scale), out_...  121 us
    pallas_call x1, Pallas kernels, stage_body(): pl.pallas_call(functools.partial(write_kernel, WRITE_PARTS, loss_scale),...  2.87 us

profile of v1, /device:TPU:97, one launch (start us, length us, event | category | flops | bytes accessed | tf_op | source)
XLA Modules:
  0.0 124.8 jit_solution(15520096868425555660)
XLA Ops:
  0.6 121.3 %shard_map.84 = (f32[1,256,1024]{2,1,0:T(8,128)}, f32[1,1024,256]{2,1,0:T(8,128)}, f32[16,256]{1,0:T(8,128)}) custom-call(bf16[4096,256]{1,0:T(8,128)(2,1)} %bitcast.2, bf16[4096,256]{1,0:T(8,128)(2,1)} %bitcast.3, bf16[1,256,1024]{2,1,0:T(8,128)(2,1)} %wu_hbm.1, bf16[1,1024,256]{2,1,0:T(8,128)(2,1)} %wd_hbm.1, f32[1,256]{1,0:T(1,128)} %gain_ref.1), custom_call_target="tpu_custom_call" | custom-call | tf_op jit(solution)/shard_map/pallas_call | solution.py:636
  121.9 2.9 %shard_map.85 = (f32[1,256,1024]{2,1,0:T(8,128)}, f32[1,1024,256]{2,1,0:T(8,128)}, f32[1,256]{1,0:T(1,128)}, f32[1]{0:T(128)}) custom-call(f32[1,256,1024]{2,1,0:T(8,128)} %get-tuple-element.7.up_hbm, f32[1,1024,256]{2,1,0:T(8,128)} %get-tuple-element.8.down_hbm, f32[16,256]{1,0:T(8,128)} %get-tuple-element.9.sums_hbm), custom_call_target="tpu_custom_call" | custom-call | tf_op jit(solution)/shard_map/pallas_call | solution.py:646
